TPU v7x, 128 devices: a whole 4x4x4 slice. The times are simulated.
128 devices in a mesh: pw: 16 (over y_hi, x, core), ka: 8 (over z, y_lo).
Axes of the slice: x: 4, y: 4 (y_hi: 2, y_lo: 2; y = y_hi * 2 + y_lo), z: 4, core: 2. Of those that a mesh axis runs over, the one named last changes fastest.
Arguments:
- waves: bfloat16 [8, 2, 32768, 256], P('ka', None, 'pw'), may hold values from -0.125 to 0.125
- projectors: bfloat16 [8, 2, 32768, 2304], P('ka', None, 'pw'), may hold values from -0.125 to 0.125
- projector_order: int32 [2304], replicated, may hold values from 0 to 2303, each once
- shift_map: int32 [32768], P('pw'), may hold values from 0 to 32767, as said below
- charges: float32 [128, 18, 18], replicated, may hold values from -0.125 to 0.125
- atom_phase: float32 [128], replicated, may hold values from -3.140625 to 3.140625
Outputs:
- margins: float32 [8, 256, 2, 256], P('ka', 'pw')
Inputs may be any that keep to these rules, and one draw needn't show every extreme that they name: `projector_order`: each projector slot once. `shift_map`: a permutation of the plane waves that maps every aligned block of 2048 plane waves onto itself.
All inputs are finite; a program needn't handle non-finite values.
Results may differ from a plain program's by a relative error of at most 0.0003.
Values may be sent and summed in bfloat16 or wider, within the bound.
A program may use at most 128 MiB of HBM per device.

v0:
```python
import jax
import jax.numpy as jnp
from jax import lax
from jax.sharding import Mesh
from jax.sharding import PartitionSpec as P

PPA = 18
PW = ("pw_0", "pw_1", "pw_2")


def from_behind(block, axis, distance):
    devices = range(lax.axis_size(axis))
    route = [((i - distance) % len(devices), i) for i in devices]
    return lax.ppermute(block, axis, route)


def split_up(array, dim, devices):
    lengths = array.shape
    pieces = array.reshape(*lengths[:dim], devices, lengths[dim] // devices, *lengths[dim + 1 :])
    return jnp.moveaxis(pieces, dim, 0)


def scatter_pairs(array, chips, core, dim):
    sizes = (lax.axis_size(chips), lax.axis_size(core))
    pieces = split_up(array, dim, sizes[0] * sizes[1])
    inside = pieces.shape[1:]
    pieces = pieces.reshape(*sizes, *inside).swapaxes(0, 1).reshape(-1, *inside)
    pieces = lax.psum_scatter(pieces, core, scatter_dimension=0, tiled=True)
    return lax.psum_scatter(pieces, chips, scatter_dimension=0, tiled=True)[0]


def sent_and_summed(array, axis, dim):
    devices = lax.axis_size(axis)
    pieces = lax.all_to_all(split_up(array, dim, devices), axis, 0, 0, tiled=True)
    return jnp.sum(pieces, axis=0)


def contract(left, right, precision=None):
    return lax.dot_general(
        left,
        right,
        (((0,), (0,)), ((), ())),
        precision=precision,
        preferred_element_type=jnp.float32,
    )


def complex_cross(left, right, precision=None):
    real = contract(left[0], right[0], precision) + contract(left[1], right[1], precision)
    imag = contract(left[0], right[1], precision) - contract(left[1], right[0], precision)
    return jnp.stack([real, imag], axis=1)


def rotate(block, phases):
    repeated = jnp.repeat(phases, PPA)
    cosine = jnp.cos(repeated)[:, None]
    sine = jnp.sin(repeated)[:, None]
    return jnp.stack([block[0] * cosine + block[1] * sine, block[1] * cosine - block[0] * sine])


def apply_charges(sym, block):
    atoms = block.shape[1] // PPA
    split = block.reshape(2, atoms, PPA, block.shape[2])
    weighted = jnp.einsum(
        "apq,raqj->rapj",
        sym,
        split,
        precision=lax.Precision.HIGHEST,
        preferred_element_type=jnp.float32,
    )
    return weighted.reshape(block.shape)


def local(waves, projectors, projector_order, shift_map, charges, atom_phase):
    wave = waves[0]
    beta = projectors[0]
    pw_dev = wave.shape[1]
    last_k = lax.axis_index("ka") == lax.axis_size("ka") - 1
    pw_index = lax.axis_index(PW)
    received = from_behind(wave, "ka", -1)
    local_map = shift_map - pw_index * pw_dev
    permuted = jnp.take(received, local_map, axis=1)
    next_wave = jnp.where(last_k, permuted, received)
    real = contract(beta[0], wave[0]) + contract(beta[1], wave[1])
    imag = contract(beta[0], wave[1]) - contract(beta[1], wave[0])
    inverse = jnp.argsort(projector_order)
    sorted_part = jnp.stack([real, imag])[:, inverse, :]
    sym = 0.5 * (charges + jnp.transpose(charges, (0, 2, 1)))
    block = scatter_pairs(sorted_part, ("pw_0", "pw_1"), "pw_2", 1)
    next_block = from_behind(block, "ka", -1)
    atom_dev = block.shape[1] // PPA
    own_phase = lax.dynamic_slice_in_dim(atom_phase, pw_index * atom_dev, atom_dev)
    own_sym = lax.dynamic_slice_in_dim(sym, pw_index * atom_dev, atom_dev, 0)
    next_block = jnp.where(last_k, rotate(next_block, own_phase), next_block)
    weighted = apply_charges(own_sym, next_block)
    result = complex_cross(wave, next_wave)
    result = result + complex_cross(block, weighted, lax.Precision.HIGHEST)
    summed = sent_and_summed(result, PW, 0)
    return summed[None]


def solution(mesh):
    torus = Mesh(mesh.devices.reshape(2, 4, 2, mesh.shape["ka"]), ("pw_0", "pw_1", "pw_2", "ka"))
    in_specs = (P("ka", None, PW, None), P("ka", None, PW, None), P(), P(PW), P(), P())
    out_specs = P("ka", PW, None, None)
    return jax.shard_map(local, mesh=torus, in_specs=in_specs, out_specs=out_specs, check_vma=False)
```

profile of v0, /device:TPU:1, one launch (start us, length us, event | category | flops | bytes accessed | tf_op | source)
XLA Modules:
  0.0 215.0 jit_solution(17378691475799144535)
XLA Ops:
  6.5 5.7 %fusion = f32[2304,256]{1,0:T(8,128)S(1)} fusion(bf16[1,2,2048,2304]{3,2,1,0:T(8,128)(2,1)} %param.7, bf16[1,2,2048,256]{3,2,1,0:T(8,128)(2,1)} %param.6), kind=kOutput, calls=%fused_computation.2 | convolution fusion | flops 2415919104 | bytes 12845056 | tf_op jit(solution)/shard_map/dot_general | solution.py:39
  12.2 4.4 %copy-done.10 = bf16[1,2,2048,2304]{3,2,1,0:T(8,128)(2,1)S(1)} copy-done((bf16[1,2,2048,2304]{3,2,1,0:T(8,128)(2,1)S(1)}, bf16[1,2,2048,2304]{3,2,1,0:T(8,128)(2,1)}, u32[]{:S(2)}) %copy-start.10) | copy-done | bytes 18874392
  16.6 2.8 %fusion.2 = f32[2304,256]{1,0:T(8,128)S(1)} fusion(bf16[1,2,2048,2304]{3,2,1,0:T(8,128)(2,1)S(1)} %copy-done.10, bf16[1,2,2048,256]{3,2,1,0:T(8,128)(2,1)S(1)} %copy-done), kind=kOutput, calls=%fused_computation.4 | convolution fusion | flops 2415919104 | bytes 12845056 | tf_op jit(solution)/shard_map/dot_general | solution.py:39
  19.4 2.9 %fusion.18 = f32[1,2304,256]{2,1,0:T(8,128)S(1)} fusion(f32[2304,256]{1,0:T(8,128)S(1)} %fusion, bf16[1,2,2048,2304]{3,2,1,0:T(8,128)(2,1)S(1)} %copy-done.10, bf16[1,2,2048,256]{3,2,1,0:T(8,128)(2,1)S(1)} %copy-done), kind=kOutput, calls=%fused_computation.19 | convolution fusion | flops 2416508928 | bytes 15204352 | tf_op jit(solution)/shard_map/dot_general | solution.py:39
  22.3 2.9 %fusion.21 = f32[1,2304,256]{2,1,0:T(8,128)S(1)} fusion(f32[2304,256]{1,0:T(8,128)S(1)} %fusion.2, bf16[1,2,2048,2304]{3,2,1,0:T(8,128)(2,1)S(1)} %copy-done.10, bf16[1,2,2048,256]{3,2,1,0:T(8,128)(2,1)S(1)} %copy-done), kind=kOutput, calls=%fused_computation.20 | convolution fusion | flops 2416508928 | bytes 15204352 | tf_op jit(solution)/shard_map/dot_general | solution.py:39
  25.1 0.3 pad_maximum_fusion
  25.5 14.4 %copy.40 = f32[2,2304,256]{2,0,1:T(2,128)} copy(f32[2,2304,256]{2,1,0:T(8,128)S(1)} %pad_maximum_fusion) | data formatting | bytes 9437184 | tf_op jit(solution)/shard_map/stack | solution.py:87
  39.9 5.8 %sort.17 = (s32[2304]{0:T(1024)}, s32[2304]{0:T(1024)S(1)}) sort(s32[2304]{0:T(1024)S(1)} %copy-done.8, s32[2304]{0:T(1024)S(1)} %iota.4), dimensions={0}, to_apply=%region_0.1 | sort | flops 27648 | bytes 36864 | tf_op jit(solution)/shard_map/jit(argsort)/sort | solution.py:86
  45.7 14.2 %gather_fusion.1 = f32[2304,2,256]{2,1,0:T(2,128)} fusion(f32[2,2304,256]{2,0,1:T(2,128)} %copy.40, s32[3072]{0:T(1024)S(1)} %pad_clamp_fusion), kind=kCustom, calls=%fused_computation.1 | custom fusion | bytes 9446400 | tf_op jit(solution)/shard_map/gather | solution.py:87
  59.9 2.9 %copy.41 = f32[2,16,144,256]{3,2,0,1:T(8,128)S(1)} copy(f32[2,16,144,256]{3,0,2,1:T(2,128)} %bitcast.107) | data formatting | bytes 9437184 | tf_op jit(solution)/shard_map/reshape | solution.py:19
  62.8 2.6 %copy.42 = f32[2,8,2,144,256]{4,3,2,1,0:T(8,128)} copy(f32[2,8,2,144,256]{4,3,2,0,1:T(8,128)S(1)} %bitcast.109) | data formatting | bytes 9437184 | tf_op jit(solution)/shard_map/transpose | solution.py:27
  65.5 14.3 %copy.77 = bf16[1,2,2048,256]{3,1,2,0:T(2,128)(2,1)} copy(bf16[1,2,2048,256]{3,2,1,0:T(8,128)(2,1)S(1)} %copy-done) | data formatting | bytes 4194304 | tf_op args[0]
  79.8 5.6 %collective-permute-start = (bf16[2,2048,256]{2,0,1:T(2,128)(2,1)}, bf16[2,2048,256]{2,0,1:T(2,128)(2,1)S(1)}, u32[]{:S(2)}, u32[]{:S(2)}) collective-permute-start(bf16[2,2048,256]{2,0,1:T(2,128)(2,1)} %bitcast.105), channel_id=1, source_target_pairs={{1,0},{2,1},{3,2},{4,3},{5,4},{6,5},{7,6},{0,7},{9,8},{10,9},{11,1... | collective-permute-start | bytes 6291464 | tf_op jit(solution)/shard_map/ppermute | solution.py:14
  86.3 53.4 %collective-permute-done = bf16[2,2048,256]{2,0,1:T(2,128)(2,1)S(1)} collective-permute-done((bf16[2,2048,256]{2,0,1:T(2,128)(2,1)}, bf16[2,2048,256]{2,0,1:T(2,128)(2,1)S(1)}, u32[]{:S(2)}, u32[]{:S(2)}) %collective-permute-start) | collective-permute-done | bytes 2097184 | tf_op jit(solution)/shard_map/ppermute | solution.py:14
  139.8 16.5 %gather_fusion = bf16[2048,2,256]{2,1,0:T(2,128)(2,1)} fusion(bf16[2,2048,256]{2,0,1:T(2,128)(2,1)S(1)} %collective-permute-done, s32[2048]{0:T(1024)S(1)} %fusion.55), kind=kCustom, calls=%fused_computation | custom fusion | bytes 4202496 | tf_op jit(solution)/shard_map/jit(_take)/gather | solution.py:82
  156.2 10.2 %broadcast_select_fusion.1 = bf16[2,2048,256]{2,0,1:T(2,128)(2,1)S(1)} fusion(bf16[2,2048,256]{2,0,1:T(2,128)(2,1)S(1)} %collective-permute-done, pred[]{:T(512)S(6)} %eq.3, bf16[2048,2,256]{2,1,0:T(2,128)(2,1)} %gather_fusion, pred[2048]{0:T(1024)(128)(4,1)S(1)} %compare_and_fusion), kind=kLoop, calls=%fused_computation.16 | loop fusion | flops 2097152 | bytes 6293505 | tf_op jit(solution)/shard_map/jit(_where)/select_n | solution.py:83
  166.4 3.0 %fusion.56 = (bf16[1,2048,256]{2,0,1:T(2,128)(2,1)S(1)}, bf16[1,2048,256]{2,0,1:T(2,128)(2,1)S(1)}) fusion(bf16[2,2048,256]{2,0,1:T(2,128)(2,1)S(1)} %broadcast_select_fusion.1), kind=kLoop, calls=%fused_computation.73 | loop fusion | bytes 4194304 | tf_op jit(solution)/shard_map/slice | solution.py:49
  169.4 1.3 copy-done.2
  170.7 0.6 fusion.25
  171.4 0.6 convolution_add_fusion.1
  171.9 0.4 reduce-scatter.5.cloned.1.call-done
  172.3 3.9 %collective-permute-start.1 = (f32[2,144,256]{2,1,0:T(8,128)}, f32[2,144,256]{2,1,0:T(8,128)S(1)}, u32[]{:S(2)}, u32[]{:S(2)}) collective-permute-start(f32[2,144,256]{2,1,0:T(8,128)} %bitcast.111), channel_id=1, source_target_pairs={{1,0},{2,1},{3,2},{4,3},{5,4},{6,5},{7,6},{0,7},{9,8},{10,9},{11,1... | collective-permute-start | bytes 884744 | tf_op jit(solution)/shard_map/ppermute | solution.py:14
  176.2 2.1 fusion.27
  178.4 0.6 convolution_subtract_fusion.1
  178.9 1.3 collective-permute-done.1
  180.6 0.5 convolution_bitcast_fusion
  181.2 0.7 fusion.54
  181.9 0.7 fusion.53
  182.5 0.7 convolution_add_fusion
  183.2 0.7 convolution_subtract_fusion
  184.0 23.5 %all_to_all.5 = f32[16,16,2,256]{3,1,2,0:T(8,128)S(1)} all-to-all(f32[16,16,2,256]{3,1,2,0:T(8,128)S(1)} %maximum_add_fusion), channel_id=1, replica_groups=mesh['pw_0'=2,'pw_1'=4,'pw_2'=2,'ka'=8] {'pw_0','pw_1','pw_2'}, dimensions={0} | all-to-all | bytes 1048576 | tf_op jit(solution)/shard_map/all_to_all | solution.py:34
  207.5 0.6 copy.50
  (46 shorter events, 1.6 us)
Async XLA Ops:
  6.5 5.7 %copy-start = (bf16[1,2,2048,256]{3,2,1,0:T(8,128)(2,1)S(1)}, bf16[1,2,2048,256]{3,2,1,0:T(8,128)(2,1)}, u32[]{:S(2)}) copy-start(bf16[1,2,2048,256]{3,2,1,0:T(8,128)(2,1)} %param.6) | copy-start | bytes 6291460
  6.5 78.8 %reduce-scatter.3.cloned.1.call-start = ((), (), s32[]{:S(2)}) async-start(), calls=%async_computation.3 | async-start | bytes 7077888 | tf_op jit(solution)/shard_map/reduce_scatter | solution.py:28
  6.5 10.1 %copy-start.10 = (bf16[1,2,2048,2304]{3,2,1,0:T(8,128)(2,1)S(1)}, bf16[1,2,2048,2304]{3,2,1,0:T(8,128)(2,1)}, u32[]{:S(2)}) copy-start(bf16[1,2,2048,2304]{3,2,1,0:T(8,128)(2,1)} %param.7) | copy-start | bytes 56623108
  25.5 14.4 %copy-start.8 = (s32[2304]{0:T(1024)S(1)}, s32[2304]{0:T(1024)}, u32[]{:S(2)}) copy-start(s32[2304]{0:T(1024)} %param.8) | copy-start | bytes 27652
  65.4 106.8 %reduce-scatter.5.cloned.1.call-start = ((), (), s32[]{:S(2)}) async-start(), calls=%async_computation.4 | async-start | bytes 2654208 | tf_op jit(solution)/shard_map/reduce_scatter | solution.py:29
  79.8 5.6 %copy-start.9 = (f32[128]{0:T(128)S(1)}, f32[128]{0:T(128)}, u32[]{:S(2)}) copy-start(f32[128]{0:T(128)} %param.11) | copy-start | bytes 1540
  79.8 6.1 %copy-start.6 = (f32[128,18,18]{0,2,1:T(8,128)S(1)}, f32[128,18,18]{0,2,1:T(8,128)}, u32[]{:S(2)}) copy-start(f32[128,18,18]{0,2,1:T(8,128)} %param.10) | copy-start | bytes 497668
  79.8 6.5 %copy-start.7 = (s32[2048]{0:T(1024)S(1)}, s32[2048]{0:T(1024)}, u32[]{:S(2)}) copy-start(s32[2048]{0:T(1024)} %param.9) | copy-start | bytes 24580
  79.8 60.0 %collective-permute-start = (bf16[2,2048,256]{2,0,1:T(2,128)(2,1)}, bf16[2,2048,256]{2,0,1:T(2,128)(2,1)S(1)}, u32[]{:S(2)}, u32[]{:S(2)}) collective-permute-start(bf16[2,2048,256]{2,0,1:T(2,128)(2,1)} %bitcast.105), channel_id=1, source_target_pairs={{1,0},{2,1},{3,2},{4,3},{5,4},{6,5},{7,6},{0,7},{9,8},{10,9},{11,1... | collective-permute-start | bytes 6291464 | tf_op jit(solution)/shard_map/ppermute | solution.py:14
  166.4 4.4 %copy-start.1 = (bf16[1,2,2048,256]{3,2,1,0:T(8,128)(2,1)S(1)}, bf16[1,2,2048,256]{3,2,1,0:T(8,128)(2,1)}, u32[]{:S(2)}) copy-start(bf16[1,2,2048,256]{3,2,1,0:T(8,128)(2,1)} %param.6) | copy-start | bytes 6291460
  169.4 1.4 copy-start.2
  169.4 2.0 copy-start.4
  172.3 6.1 %copy-start.3 = (bf16[1,2048,256]{2,0,1:T(2,128)(2,1)S(1)}, bf16[1,2048,256]{2,0,1:T(2,128)(2,1)}, u32[]{:S(2)}) copy-start(bf16[1,2048,256]{2,0,1:T(2,128)(2,1)} %copy-done.2) | copy-start | bytes 3145732
  172.3 7.9 %collective-permute-start.1 = (f32[2,144,256]{2,1,0:T(8,128)}, f32[2,144,256]{2,1,0:T(8,128)S(1)}, u32[]{:S(2)}, u32[]{:S(2)}) collective-permute-start(f32[2,144,256]{2,1,0:T(8,128)} %bitcast.111), channel_id=1, source_target_pairs={{1,0},{2,1},{3,2},{4,3},{5,4},{6,5},{7,6},{0,7},{9,8},{10,9},{11,1... | collective-permute-start | bytes 884744 | tf_op jit(solution)/shard_map/ppermute | solution.py:14
  178.9 2.3 %copy-start.5 = (f32[1,2,144,256]{3,2,1,0:T(8,128)S(1)}, f32[1,2,144,256]{3,2,1,0:T(8,128)}, u32[]{:S(2)}) copy-start(f32[1,2,144,256]{3,2,1,0:T(8,128)} %reduce-scatter.5.cloned.1.call-done) | copy-start | bytes 884740
Sparse Core Ops, SparseCore 0:
  65.6 18.7 reduce-scatter.2
  88.2 84.0 reduce-scatter.4
where the time goes:
time: 215 us
  local copies, waits for them, and re-layouts  75.3 us (35%)
  waiting for transfers between devices  55.1 us (26%)
  blocking collectives  23.5 us (11%)
  matrix products  21.1 us (10%)
  other arithmetic  16.7 us (8%)
  between operations  13.7 us (6%)
  starting transfers between devices  9.58 us (4%)
    ppermute x2, waiting for transfers between devices, from_behind(): return lax.ppermute(block, axis, route)  54.7 us
    all_to_all x1, blocking collectives, sent_and_summed(): lax.all_to_all(split_up(array, dim, devices), axis, 0, 0, tiled=True)  23.5 us
    dot_general x12, matrix products, contract(): lax.dot_general(left, right, (((0,), (0,)), ((), ())), precision=precisio...  20.6 us
    unnamed x24, local copies, waits for them, and re-layouts  20.1 us
    gather x1, local copies, waits for them, and re-layouts, local(): permuted = jnp.take(received, local_map, axis=1)  16.5 us
    another operation x1, local copies, waits for them, and re-layouts, local(): sorted_part = jnp.stack([real, imag])[:, inverse, :]  14.4 us
    gather x1, local copies, waits for them, and re-layouts, local(): sorted_part = jnp.stack([real, imag])[:, inverse, :]  14.2 us
    select_n x1, other arithmetic, local(): next_wave = jnp.where(last_k, permuted, received)  10.2 us
  transfers between devices with their start and end apart: 4, of which 3 were waited for; matrix products, arithmetic and copies ran while one was open for 23% of the time, Pallas kernels for 0%

commit v1 on v0

v1 whole, which is shorter than its diff:
```python
import jax
import jax.numpy as jnp
from jax import lax
from jax.experimental import pallas as pl
from jax.experimental.pallas import tpu as pltpu
from jax.sharding import PartitionSpec as P

MESH = pl.DeviceIdType.MESH
HIGH = lax.Precision.HIGHEST
F32 = jnp.float32
BF16 = jnp.bfloat16

NPW = 2048
NB = 256
PPA = 18
NPROJ = 2304
COLS = 256
STEPS = NPROJ // COLS
PARTS = 2
SLOTS = 72
ROWS = 4 * SLOTS
WCH = 8
WROWS = NPW // WCH


def dot(a, b, dims=((1,), (0,)), precision=None):
    return lax.dot_general(a, b, (dims, ((), ())), precision=precision, preferred_element_type=F32)


def iota(shape, dim):
    return lax.broadcasted_iota(jnp.int32, shape, dim)


def kernel(
    order_ref, shift_ref, phase_ref, charges_ref, waves_ref, proj_ref, out_ref,
    wv, lt, beta, pu, ps, crecv, far, near, ydst, nxt, wsend, wnext,
    colb, invv, invs, chv, sym, plane, stage, oc, ocore, orecv, onehot,
    load_sem, beta_sem, misc_sem, core_s, core_r, x_s, far_r, near_r, y_s, y_r, n_s, n_r,
    w_s, w_r, oc_s, oc_r, o_s, o_r,
):
    me = lax.axis_index("pw")
    ka = lax.axis_index("ka")
    core = lax.rem(me, 2)
    j = me // 2
    x = lax.rem(j, 4)
    h = j // 4
    oh = 1 - h
    right = lax.rem(x + 1, 4)
    left = lax.rem(x + 3, 4)
    across = lax.rem(x + 2, 4)
    before = lax.rem(ka + 7, 8)
    after = lax.rem(ka + 1, 8)
    first = ka == 0
    last = ka == 7

    def pw_of(hh, xx, cc):
        return (hh * 4 + xx) * 2 + cc

    def send(src, dst, s, r, pw, k):
        return pltpu.make_async_remote_copy(src_ref=src, dst_ref=dst, send_sem=s, recv_sem=r, device_id=(pw, k), device_id_type=MESH)

    load = pltpu.make_async_copy(waves_ref.at[0], wv, load_sem)
    load.start()

    def beta_copy(i):
        src = proj_ref.at[0, :, :, pl.ds(pl.multiple_of(i * COLS, COLS), COLS)]
        return pltpu.make_async_copy(src, beta.at[i], beta_sem.at[i])

    for i in range(STEPS):
        beta_copy(i).start()
    ch_copy = pltpu.make_async_copy(charges_ref.at[pl.ds(8 * me, 8)], chv, misc_sem.at[0])
    ch_copy.start()

    barrier = pltpu.get_barrier_semaphore()
    for d in range(1, 16):
        pl.semaphore_signal(barrier, inc=1, device_id=(lax.rem(me + d, 16), ka), device_id_type=MESH)
    for k in (before, after):
        pl.semaphore_signal(barrier, inc=1, device_id=(me, k), device_id_type=MESH)
    pl.semaphore_wait(barrier, 17)

    def w_copy(c, src):
        return send(src, wnext.at[:, pl.ds(pl.multiple_of(c * WROWS, WROWS), WROWS), :], w_s.at[c], w_r.at[c], me, before)

    def rows_of(ref, c):
        return ref.at[:, pl.ds(pl.multiple_of(c * WROWS, WROWS), WROWS), :]

    @pl.when(jnp.logical_not(first))
    def _():
        for c in range(WCH):
            w_copy(c, waves_ref.at[0, :, pl.ds(c * WROWS, WROWS), :]).start()

    load.wait()

    @pl.when(first)
    def _():
        def piece(c, _):
            for half in range(WROWS // 128):
                row = shift_ref[pl.ds(c * (WROWS // 128) + half, 1), :] - me * NPW
                want = jnp.broadcast_to(row.astype(F32), (128, 128)).T
                for t in range(NPW // 128):
                    have = (iota((128, 128), 1) + 128 * t).astype(F32)
                    onehot[:, 128 * t : 128 * (t + 1)] = jnp.where(want == have, 1.0, 0.0).astype(BF16)
                at = pl.ds(pl.multiple_of(c * WROWS + half * 128, 128), 128)
                for r in range(2):
                    wsend[r, at, :] = dot(onehot[...], wv[r]).astype(BF16)
            w_copy(c, rows_of(wsend, c)).start()
            return 0

        lax.fori_loop(0, WCH, piece, 0)

    for r in range(NPROJ // 128):
        row = order_ref[pl.ds(r, 1), :].astype(F32)
        colb[pl.ds(128 * r, 128), :] = jnp.broadcast_to(row, (128, 128)).T

    def invert(b, _):
        slot = (iota((NPROJ, 128), 1) + 128 * b).astype(F32)
        hit = jnp.where(colb[...] == slot, (iota((NPROJ, 128), 0) * 4).astype(F32), 0.0)
        found = jnp.sum(hit, axis=0, keepdims=True).astype(jnp.int32)
        invv[pl.ds(b, 1), :] = jnp.clip(found, 0, 4 * (NPROJ - 1))
        return 0

    lax.fori_loop(0, NPROJ // 128, invert, 0)
    inv_copy = pltpu.make_async_copy(invv, invs, misc_sem.at[1])
    inv_copy.start()

    for c in range(8):
        g = slice(256 * c, 256 * (c + 1))
        gi = slice(NPW + 256 * c, NPW + 256 * (c + 1))
        re = wv[0, g, :].T
        im = wv[1, g, :].T
        lt[0:NB, g] = re
        lt[0:NB, gi] = im
        lt[NB:, g] = im
        lt[NB:, gi] = -re

    def project(i, _):
        beta_copy(i).wait()
        acc = dot(lt[...], beta[i].reshape(2 * NPW, COLS))
        for q in range(4):
            pu[pl.ds(pl.multiple_of(4 * COLS * i, 8) + q, COLS, stride=4), :] = acc[128 * q : 128 * (q + 1), :].T
        return 0

    lax.fori_loop(0, STEPS, project, 0)
    inv_copy.wait()

    def gather(c, cr):
        def block(b, _):
            s0 = (2 * b + cr) * 2 * SLOTS + c * SLOTS

            def body(i, _):
                for u in range(8):
                    n = i * 8 + u
                    s = s0 + n
                    r = invs[s >> 7, s & 127]
                    ps[c, cr, b, pl.ds(pl.multiple_of(4 * n, 4), 4), :] = pu[pl.ds(r, 4), :]
                return 0

            return lax.fori_loop(0, SLOTS // 8, body, 0)

        lax.fori_loop(0, 8, block, 0)

    pw_core = pw_of(h, x, 1 - core)
    pw_right = pw_of(h, right, core)
    pw_left = pw_of(h, left, core)
    pw_y = pw_of(oh, x, core)

    def core_copy(c):
        return send(ps.at[c, 1 - core], crecv.at[c], core_s.at[c], core_r.at[c], pw_core, ka)

    for c in range(PARTS):
        gather(c, 1 - core)
        core_copy(c).start()
        gather(c, core)

    def block_of(hh, xx):
        return hh * 4 + xx

    def mine(c, b):
        return ps.at[c, core, b]

    def far_copy(c, d):
        return send(mine(c, block_of(d, across)), far.at[c, d], x_s.at[c, d], far_r.at[c, d], (pw_right, pw_left)[d], ka)

    def near_copy(c, d, hh):
        return send(
            mine(c, block_of(hh, (right, left)[d])), near.at[c, d, hh], x_s.at[c, 2 + 2 * d + hh], near_r.at[c, d, hh],
            (pw_right, pw_left)[d], ka,
        )

    def add_core(c, b):
        ps[c, core, b] += crecv[c, b]

    for c in range(PARTS):
        core_copy(c).wait_recv()
        for d in range(2):
            add_core(c, block_of(d, across))
            far_copy(c, d).start()
        for d in range(2):
            add_core(c, block_of(1 - d, (right, left)[d]))
            near_copy(c, d, 1 - d).start()
        for d in range(2):
            add_core(c, block_of(d, (right, left)[d]))
        for hh in range(2):
            add_core(c, block_of(hh, x))
    for c in range(PARTS):
        for d in range(2):
            far_copy(c, d).wait_recv()
            ps[c, core, block_of(d, (right, left)[d])] += far[c, d]
            near_copy(c, d, d).start()

    def y_copy(c):
        return send(mine(c, block_of(oh, x)), ydst.at[c], y_s.at[c], y_r.at[c], pw_y, ka)

    def n_copy(c):
        return send(mine(c, block_of(h, x)), nxt.at[c], n_s.at[c], n_r.at[c], me, before)

    for c in range(PARTS):
        for d in range(2):
            for hh in range(2):
                near_copy(c, d, hh).wait_recv()
        ps[c, core, block_of(oh, x)] += near[c, 0, oh] + near[c, 1, oh]
        y_copy(c).start()
        ps[c, core, block_of(h, x)] += near[c, 0, h] + near[c, 1, h]
    for c in range(PARTS):
        y_copy(c).wait_recv()
        ps[c, core, block_of(h, x)] += ydst[c]
        n_copy(c).start()

    ch_copy.wait()
    slot_r = iota((SLOTS, PPA), 0)
    chan_c = iota((SLOTS, PPA), 1)
    atom_row = ((iota((SLOTS, SLOTS), 0).astype(F32) + 0.5) * (1.0 / PPA)).astype(jnp.int32)
    atom_col = ((iota((SLOTS, SLOTS), 1).astype(F32) + 0.5) * (1.0 / PPA)).astype(jnp.int32)
    same = atom_row == atom_col
    spread = jnp.zeros((PPA, SLOTS), F32)
    for a in range(SLOTS // PPA):
        spread += jnp.where(iota((PPA, SLOTS), 1) == iota((PPA, SLOTS), 0) + PPA * a, 1.0, 0.0)
    for c in range(PARTS):
        flat = jnp.zeros((SLOTS, PPA), F32)
        for a in range(SLOTS // PPA):
            pick = jnp.where(slot_r == chan_c + PPA * a, 1.0, 0.0).astype(F32)
            charge = chv[c * (SLOTS // PPA) + a]
            flat += dot(pick, charge, precision=HIGH) + dot(pick, charge, ((1,), (1,)), HIGH)
        sym[c] = jnp.where(same, dot(0.5 * flat, spread, precision=HIGH), 0.0)

    def wide(ref, lo):
        return jnp.concatenate([ref[pl.ds(lo, SLOTS, stride=4), :], ref[pl.ds(lo + 1, SLOTS, stride=4), :]], axis=1)

    colb[0:128, :] = jnp.broadcast_to(phase_ref[...], (128, 128)).T
    own = colb[pl.ds(pl.multiple_of(8 * me, 8), 8), :]
    cosine = jnp.cos(own)
    sine = jnp.sin(own)

    total = jnp.zeros((NB, 2 * NB), F32)
    for c in range(PARTS):
        n_copy(c).wait_recv()
        nr = wide(nxt.at[c], 0)
        ni = wide(nxt.at[c], 2)
        repeat = jnp.where(((iota((SLOTS, 8), 0).astype(F32) + 0.5) * (1.0 / PPA)).astype(jnp.int32) + c * (SLOTS // PPA) == iota((SLOTS, 8), 1), 1.0, 0.0)
        cc = dot(repeat, cosine, precision=HIGH)
        sc = dot(repeat, sine, precision=HIGH)
        cc = jnp.where(last, jnp.concatenate([cc, cc], axis=1), 1.0)
        sc = jnp.where(last, jnp.concatenate([sc, sc], axis=1), 0.0)
        turned = jnp.concatenate([nr * cc + ni * sc, ni * cc - nr * sc], axis=1)
        weighted = dot(sym[c], turned, precision=HIGH)
        wr = weighted[:, :NB]
        wi = weighted[:, NB:]
        pk = ps.at[c, core, block_of(h, x)]
        pr = wide(pk, 0)
        pi = wide(pk, 2)
        total += dot(pr, jnp.concatenate([wr, wi], axis=1), ((0,), (0,)), HIGH)
        total += dot(pi, jnp.concatenate([wi, -wr], axis=1), ((0,), (0,)), HIGH)
    stage[...] = total

    plane[...] = jnp.zeros_like(plane)

    def product(i, _):
        w_copy(2 * i, rows_of(wsend, 2 * i)).wait_recv()
        w_copy(2 * i + 1, rows_of(wsend, 2 * i + 1)).wait_recv()
        g = pl.ds(pl.multiple_of(2 * WROWS * i, 128), 2 * WROWS)
        gi = pl.ds(pl.multiple_of(NPW + 2 * WROWS * i, 128), 2 * WROWS)
        plane[...] += dot(lt[:, g], wnext[0, g, :]) + dot(lt[:, gi], wnext[1, g, :])
        return 0

    lax.fori_loop(0, WCH // 2, product, 0)

    for p in range(16):
        rows = slice(16 * p, 16 * (p + 1))
        oc[p % 2, p // 2, 0] = stage[rows, :NB] + plane[rows, :]
        oc[p % 2, p // 2, 1] = stage[rows, NB:] - plane[NB + 16 * p : NB + 16 * (p + 1), :]
    o_core = send(oc.at[1 - core], ocore, oc_s, oc_r, pw_core, ka)
    o_core.start()
    o_core.wait_recv()
    for b in range(8):
        oc[core, b] += ocore[b]

    def o_copy(d):
        to = lax.rem(j + d, 8)
        return send(oc.at[core, to], orecv.at[d], o_s.at[d], o_r.at[d], 2 * to + core, ka)

    for d in range(1, 8):
        o_copy(d).start()
    result = oc[core, j]
    for d in range(1, 8):
        o_copy(d).wait_recv()
        result += orecv[d]
    out_ref[0, :, 0, :] = result[0]
    out_ref[0, :, 1, :] = result[1]

    o_core.wait_send()
    for d in range(1, 8):
        o_copy(d).wait_send()
    for c in range(WCH):
        w_copy(c, rows_of(wsend, c)).wait_send()
    for c in range(PARTS):
        core_copy(c).wait_send()
        y_copy(c).wait_send()
        n_copy(c).wait_send()
        for d in range(2):
            far_copy(c, d).wait_send()
            for hh in range(2):
                near_copy(c, d, hh).wait_send()


def local(waves, projectors, projector_order, shift_map, charges, atom_phase):
    vmem = pl.BlockSpec(memory_space=pltpu.VMEM)
    hbm = pl.BlockSpec(memory_space=pl.ANY)
    dma = pltpu.SemaphoreType.DMA
    return pl.pallas_call(
        kernel,
        out_shape=jax.ShapeDtypeStruct((1, 16, 2, NB), F32),
        in_specs=[vmem, vmem, vmem, hbm, hbm, hbm],
        out_specs=vmem,
        scratch_shapes=[
            pltpu.VMEM((2, NPW, NB), BF16),
            pltpu.VMEM((2 * NB, 2 * NPW), BF16),
            pltpu.VMEM((STEPS, 2, NPW, COLS), BF16),
            pltpu.VMEM((4 * NPROJ, 128), F32),
            pltpu.VMEM((PARTS, 2, 8, ROWS, 128), F32),
            pltpu.VMEM((PARTS, 8, ROWS, 128), F32),
            pltpu.VMEM((PARTS, 2, ROWS, 128), F32),
            pltpu.VMEM((PARTS, 2, 2, ROWS, 128), F32),
            pltpu.VMEM((PARTS, ROWS, 128), F32),
            pltpu.VMEM((PARTS, ROWS, 128), F32),
            pltpu.VMEM((2, NPW, NB), BF16),
            pltpu.VMEM((2, NPW, NB), BF16),
            pltpu.VMEM((NPROJ, 128), F32),
            pltpu.VMEM((NPROJ // 128, 128), jnp.int32),
            pltpu.SMEM((NPROJ // 128, 128), jnp.int32),
            pltpu.VMEM((8, PPA, PPA), F32),
            pltpu.VMEM((PARTS, SLOTS, SLOTS), F32),
            pltpu.VMEM((2 * NB, NB), F32),
            pltpu.VMEM((NB, 2 * NB), F32),
            pltpu.VMEM((2, 8, 2, 16, NB), F32),
            pltpu.VMEM((8, 2, 16, NB), F32),
            pltpu.VMEM((8, 2, 16, NB), F32),
            pltpu.VMEM((128, NPW), BF16),
            dma, dma((STEPS,)), dma((2,)),
            dma((PARTS,)), dma((PARTS,)),
            dma((PARTS, 6)), dma((PARTS, 2)), dma((PARTS, 2, 2)),
            dma((PARTS,)), dma((PARTS,)), dma((PARTS,)), dma((PARTS,)),
            dma((WCH,)), dma((WCH,)),
            dma, dma, dma((8,)), dma((8,)),
        ],
        compiler_params=pltpu.CompilerParams(collective_id=0, has_side_effects=True, vmem_limit_bytes=64 * 1024 * 1024 - 65536),
    )(
        projector_order.reshape(NPROJ // 128, 128),
        shift_map.reshape(NPW // 128, 128),
        atom_phase.reshape(1, 128),
        charges,
        waves,
        projectors,
    )


def solution(mesh):
    in_specs = (P("ka", None, "pw", None), P("ka", None, "pw", None), P(), P("pw"), P(), P())
    out_specs = P("ka", "pw", None, None)
    return jax.shard_map(local, mesh=mesh, in_specs=in_specs, out_specs=out_specs, check_vma=False)
```

time: 215 us -> 90.4 us (0.42)
  Pallas kernels: 0 us -> 86.1 us
  local copies, waits for them, and re-layouts: 75.3 us -> 3.96 us
  waiting for transfers between devices: 55.1 us -> 0 us
  blocking collectives: 23.5 us -> 0 us
  matrix products: 21.1 us -> 0 us
  other arithmetic: 16.7 us -> 0 us
  between operations: 13.7 us -> 0.01 us
  starting transfers between devices: 9.58 us -> 0 us
    pallas_call x0 -> x1, Pallas kernels: none -> 86.1 us  [local(): pl.pallas_call(kernel, out_shape=jax.ShapeDtypeStruct((1, 16, 2, NB), F32...]
    ppermute x2 -> x0, waiting for transfers between devices: 54.7 us -> none  [from_behind(): return lax.ppermute(block, axis, route)]
    gather x2 -> x0, local copies, waits for them, and re-layouts: 30.7 us -> none  [the longest x1 16.5 us: local(): permuted = jnp.take(received, local_map, axis=1)]
    all_to_all x1 -> x0, blocking collectives: 23.5 us -> none  [sent_and_summed(): lax.all_to_all(split_up(array, dim, devices), axis, 0, 0, tiled=True)]
    dot_general x13 -> x0, matrix products: 21.1 us -> none  [the longest x12 20.6 us: contract(): lax.dot_general(left, right, (((0,), (0,)), ((), ())), precision=precisio...]
    unnamed x24 -> x2, local copies, waits for them, and re-layouts: 20.1 us -> 3.96 us
    another operation x1 -> x0, local copies, waits for them, and re-layouts: 14.4 us -> none  [local(): sorted_part = jnp.stack([real, imag])[:, inverse, :]]
    select_n x3 -> x0, other arithmetic: 10.2 us -> none  [the longest x1 10.2 us: local(): next_wave = jnp.where(last_k, permuted, received)]
  transfers between devices with their start and end apart: 4 -> 0, of which waited for: 3 -> 0; matrix products, arithmetic and copies ran while one was open for 23% -> 0% of each run, Pallas kernels for 0% -> 0%
where the time goes in v1:
time: 90.4 us; the launch traced here: 90.1 us
  Pallas kernels  86.1 us (95%)
  local copies, waits for them, and re-layouts  3.96 us (4%)
    pallas_call x1, Pallas kernels, local(): pl.pallas_call(kernel, out_shape=jax.ShapeDtypeStruct((1, 16, 2, NB), F32...  86.1 us
    unnamed x2, local copies, waits for them, and re-layouts  3.96 us

profile of v1, /device:TPU:1, one launch (start us, length us, event | category | flops | bytes accessed | tf_op | source)
XLA Modules:
  0.0 90.1 jit_solution(1045812955554811562)
XLA Ops:
  0.0 2.6 %copy.7.charges_ref = f32[128,18,18]{2,1,0:T(8,128)} copy(f32[128,18,18]{0,2,1:T(8,128)} %param.10) | data formatting | bytes 331776 | tf_op args[4]
  2.6 86.1 %shard_map.64 = f32[1,16,2,256]{3,2,1,0:T(2,128)} custom-call(s32[18,128]{1,0:T(8,128)} %bitcast.3, s32[16,128]{1,0:T(8,128)} %bitcast.4, f32[1,128]{1,0:T(1,128)} %bitcast.5, f32[128,18,18]{2,1,0:T(8,128)} %copy.7.charges_ref, bf16[1,2,2048,256]{3,2,1,0:T(8,128)(2,1)} %waves_ref.1, bf16[1,2,2048,2304]{3,2,1,0:T(8,128)(2,1)} %proj_ref.1), custom_call_target="tpu_custom_call" | custom-call | tf_op jit(solution)/shard_map/pallas_call | solution.py:329
  88.7 1.4 %copy.9 = f32[1,16,2,256]{3,2,1,0:T(2,128)} copy(f32[1,16,2,256]{3,2,1,0:T(2,128)} %shard_map.64) | data formatting | bytes 65536

commit v2 on v1

v2 whole, which is shorter than its diff:
```python
import jax
import jax.numpy as jnp
from jax import lax
from jax.experimental import pallas as pl
from jax.experimental.pallas import tpu as pltpu
from jax.sharding import PartitionSpec as P

MESH = pl.DeviceIdType.MESH
HIGH = lax.Precision.HIGHEST
F32 = jnp.float32
BF16 = jnp.bfloat16

NPW = 2048
NB = 256
PPA = 18
NPROJ = 2304
COLS = 256
STEPS = NPROJ // COLS
PARTS = 2
HALF = NB // PARTS
SLOTS = 144
SUB = 1
ROWS = 2 * SLOTS
OWN = NPW // 2
WCH = 8
WROWS = OWN // WCH
XCH = 4
EXTRA = OWN // 2
SPLIT = 6


def dot(a, b, dims=((1,), (0,)), precision=None):
    return lax.dot_general(a, b, (dims, ((), ())), precision=precision, preferred_element_type=F32)


def iota(shape, dim):
    return lax.broadcasted_iota(jnp.int32, shape, dim)


def kernel(
    order_ref, shift_ref, phase_ref, charges_ref, waves_ref, proj_ref, out_ref,
    wv, lt, beta, pu, ps, crecv, far, near, ydst, nxt, pk, xw, yw, ew, es, lp,
    colb, acc, invv, invs, sym, turn, bra, ket, plane, stage, oc, ocore, orecv, onehot,
    load_sem, beta_sem, inv_sem, core_s, core_r, x_s, far_r, near_r, y_s, y_r, n_s, n_r,
    w_s, w_r, f_s, f_r, e_s, e_r, oc_s, oc_r, o_s, o_r,
):
    me = lax.axis_index("pw")
    ka = lax.axis_index("ka")
    core = lax.rem(me, 2)
    j = me // 2
    x = lax.rem(j, 4)
    h = j // 4
    oh = 1 - h
    right = lax.rem(x + 1, 4)
    left = lax.rem(x + 3, 4)
    across = lax.rem(x + 2, 4)
    before = lax.rem(ka + 7, 8)
    after = lax.rem(ka + 1, 8)
    first = ka == 0
    last = ka == 7
    odd = lax.rem(ka, 2)
    partner = ka + 1 - 2 * odd
    beyond = lax.rem(ka + 2 + 4 * odd, 8)
    sent = OWN * (1 - odd)
    kept = OWN * odd

    def pw_of(hh, xx, cc):
        return (hh * 4 + xx) * 2 + cc

    def send(src, dst, s, r, pw, k):
        return pltpu.make_async_remote_copy(src_ref=src, dst_ref=dst, send_sem=s, recv_sem=r, device_id=(pw, k), device_id_type=MESH)

    load = pltpu.make_async_copy(waves_ref.at[0], wv, load_sem)
    load.start()

    def beta_copy(i):
        src = proj_ref.at[0, :, :, pl.ds(pl.multiple_of(i * COLS, COLS), COLS)]
        return pltpu.make_async_copy(src, beta.at[i], beta_sem.at[i])

    for i in range(2):
        beta_copy(i).start()

    pw_y = pw_of(oh, x, core)
    barrier = pltpu.get_barrier_semaphore()
    peers = [(lax.rem(me + d, 16), ka) for d in range(1, 16)]
    peers += [(me, lax.rem(ka + d, 8)) for d in (2, 6)]
    peers += [(2 * lax.rem(j + d, 8) + core, k) for d in range(8) for k in (before, after)]
    for peer in peers:
        pl.semaphore_signal(barrier, inc=1, device_id=peer, device_id_type=MESH)

    order = jnp.concatenate([order_ref[pl.ds(r, 1), :] for r in range(NPROJ // 128)], axis=1)
    column = iota((SLOTS, NPROJ), 1)
    match_hi = (order >> 4) == iota((SLOTS, NPROJ), 0)
    match_lo = jnp.where((order & 15) == iota((16, NPROJ), 0), 1.0, 0.0).astype(BF16)
    digit_hi = jnp.where(match_hi, (column >> 7).astype(F32), 0.0).astype(BF16)
    digit_lo = jnp.where(match_hi, (column & 127).astype(F32), 0.0).astype(BF16)
    found = dot(digit_hi, match_lo, ((1,), (1,))) * 128.0 + dot(digit_lo, match_lo, ((1,), (1,)))
    invv[...] = jnp.clip(2 * found.astype(jnp.int32), 0, 2 * (NPROJ - 1))
    inv_copy = pltpu.make_async_copy(invv, invs, inv_sem)
    inv_copy.start()

    load.wait()
    for i in range(2, STEPS):
        beta_copy(i).start()

    for c in range(8):
        g = slice(256 * c, 256 * (c + 1))
        gi = slice(NPW + 256 * c, NPW + 256 * (c + 1))
        re = wv[0, g, :].T
        im = wv[1, g, :].T
        for p in range(PARTS):
            bands = slice(HALF * p, HALF * (p + 1))
            lt[NB * p : NB * p + HALF, g] = re[bands]
            lt[NB * p : NB * p + HALF, gi] = im[bands]
            lt[NB * p + HALF : NB * (p + 1), g] = im[bands]
            lt[NB * p + HALF : NB * (p + 1), gi] = -re[bands]

    pl.semaphore_wait(barrier, len(peers))

    def piece(ref, c):
        return ref.at[:, pl.ds(c * WROWS, WROWS), :]

    def w_copy(c):
        src = waves_ref.at[0, :, pl.ds(pl.multiple_of(sent + c * WROWS, WROWS), WROWS), :]
        return send(src, piece(xw, c), w_s.at[c], w_r.at[c], me, partner)

    def f_copy(c):
        return send(piece(xw, c), piece(yw, c), f_s.at[c], f_r.at[c], me, beyond)

    def to_last(c):
        return send(piece(es, c), piece(yw, c), e_s.at[c], f_r.at[c], me, before)

    def to_first(c):
        src = waves_ref.at[0, :, pl.ds(OWN + EXTRA + c * WROWS, WROWS), :]
        return send(src, piece(ew, c), e_s.at[c], e_r.at[c], me, after)

    for c in range(WCH):
        w_copy(c).start()

    @pl.when(last)
    def _():
        for c in range(XCH):
            to_first(c).start()

    def forward(lo, hi):
        for c in range(lo, hi):
            w_copy(c).wait_recv()

        @pl.when(ka != 1)
        def _():
            for c in range(lo, hi):
                f_copy(c).start()

    def choose(group):
        row = shift_ref[pl.ds(group, 1), :] - me * NPW
        want = jnp.broadcast_to(row.astype(F32), (128, 128)).T
        for t in range(NPW // 128):
            have = (iota((128, 128), 1) + 128 * t).astype(F32)
            onehot[:, 128 * t : 128 * (t + 1)] = jnp.where(want == have, 1.0, 0.0).astype(BF16)

    def extra_first():
        @pl.when(first)
        def _():
            def body(t, _):
                choose(OWN // 128 + t)
                for r in range(2):
                    es[r, pl.ds(pl.multiple_of(128 * t, 128), 128), :] = dot(onehot[...], wv[r]).astype(BF16)
                return 0

            lax.fori_loop(0, EXTRA // 128, body, 0)
            for c in range(XCH):
                to_last(c).start()

    def permute_first():
        @pl.when(first)
        def _():
            def body(t, _):
                choose(t + jnp.where(t >= OWN // 128, EXTRA // 128, 0))
                got = dot(lt[:, 0:NPW], onehot[...], ((1,), (1,))).astype(BF16)
                at = pl.multiple_of(128 * t, 128)
                lp[:, pl.ds(at, 128)] = got
                for p in range(PARTS):
                    lo = NB * p
                    lp[lo : lo + HALF, pl.ds(OWN + EXTRA + at, 128)] = got[lo + HALF : lo + NB]
                    lp[lo + HALF : lo + NB, pl.ds(OWN + EXTRA + at, 128)] = -got[lo : lo + HALF]
                return 0

            lax.fori_loop(0, (OWN + EXTRA) // 128, body, 0)

    def put(c, i):
        for q in range(2):
            pu[c, pl.ds(pl.multiple_of(2 * COLS * i, 8) + q, COLS, stride=2), :] = acc[HALF * q : HALF * (q + 1), :].T

    def project(c, lo, hi):
        def body(i, _):
            if c == 0:
                beta_copy(i).wait()
            put(c, jnp.maximum(i - 1, lo))
            acc[...] = dot(lt[NB * c : NB * (c + 1), :], beta[i].reshape(2 * NPW, COLS))
            return 0

        lax.fori_loop(lo, hi, body, 0)
        put(c, hi - 1)

    def gather(c, cr):
        def block(b, _):
            dst = ps.at[c, cr, b]

            def body(i, _):
                rows = [invs[9 * (2 * b + cr) + i, u] for u in range(16)]
                got = [pu[c, pl.ds(r, 2), :] for r in rows]
                for u in range(16):
                    dst[pl.ds(pl.multiple_of(32 * i, 32) + 2 * u, 2), :] = got[u]
                return 0

            return lax.fori_loop(0, SLOTS // 16, body, 0)

        lax.fori_loop(0, 8, block, 0)

    pw_core = pw_of(h, x, 1 - core)
    pw_right = pw_of(h, right, core)
    pw_left = pw_of(h, left, core)
    def core_copy(c):
        return send(ps.at[c, 1 - core], crecv.at[c], core_s.at[c], core_r.at[c], pw_core, ka)

    def spread_out(c):
        gather(c, 1 - core)
        core_copy(c).start()
        gather(c, core)

    def block_of(hh, xx):
        return hh * 4 + xx

    def sub(ref, e):
        return ref.at[pl.ds(e * (ROWS // SUB), ROWS // SUB), :]

    def mine(c, e, b):
        return sub(ps.at[c, core, b], e)

    def far_copy(c, e, d):
        return send(
            mine(c, e, block_of(d, across)), sub(far.at[c, d], e), x_s.at[c, e, d], far_r.at[c, e, d], (pw_right, pw_left)[d], ka
        )

    def near_copy(c, e, d, hh):
        return send(
            mine(c, e, block_of(hh, (right, left)[d])), sub(near.at[c, d, hh], e), x_s.at[c, e, 2 + 2 * d + hh],
            near_r.at[c, e, d, hh], (pw_right, pw_left)[d], ka,
        )

    def add_core(c, b):
        ps[c, core, b] += crecv[c, b]

    def ring_start(c):
        core_copy(c).wait_recv()
        for d in range(2):
            add_core(c, block_of(d, across))
            for e in range(SUB):
                far_copy(c, e, d).start()
        for d in range(2):
            add_core(c, block_of(1 - d, (right, left)[d]))
            for e in range(SUB):
                near_copy(c, e, d, 1 - d).start()
        for d in range(2):
            add_core(c, block_of(d, (right, left)[d]))
        for hh in range(2):
            add_core(c, block_of(hh, x))

    def add(c, e, b, ref):
        at = pl.ds(e * (ROWS // SUB), ROWS // SUB)
        total = ps[c, core, b, at, :]
        for one in ref:
            total += one[at, :]
        ps[c, core, b, at, :] = total

    def ring_rest(c):
        for e in range(SUB):
            for d in range(2):
                far_copy(c, e, d).wait_recv()
                add(c, e, block_of(d, (right, left)[d]), [far.at[c, d]])
                near_copy(c, e, d, d).start()

    def y_copy(c, e):
        return send(mine(c, e, block_of(oh, x)), sub(ydst.at[c], e), y_s.at[c, e], y_r.at[c, e], pw_y, ka)

    def n_copy(c, e, d):
        return send(
            mine(c, e, block_of((h, oh)[d], x)), sub(nxt.at[c, d], e), n_s.at[c, e, d], n_r.at[c, e, d], (me, pw_y)[d], before
        )

    def ring_end(c):
        for e in range(SUB):
            for d in range(2):
                for hh in range(2):
                    near_copy(c, e, d, hh).wait_recv()
            add(c, e, block_of(oh, x), [near.at[c, 0, oh], near.at[c, 1, oh]])
            y_copy(c, e).start()
            n_copy(c, e, 1).start()
            add(c, e, block_of(h, x), [near.at[c, 0, h], near.at[c, 1, h]])
            n_copy(c, e, 0).start()

    acc[...] = jnp.zeros_like(acc)
    project(0, 0, STEPS)
    inv_copy.wait()
    spread_out(0)
    forward(0, 2)
    project(1, 0, SPLIT)
    ring_start(0)
    project(1, SPLIT, STEPS)
    forward(2, 4)
    spread_out(1)
    extra_first()
    ring_rest(0)
    forward(4, 6)
    ring_start(1)

    atom_row = ((iota((SLOTS, SLOTS), 0).astype(F32) + 0.5) * (1.0 / PPA)).astype(jnp.int32)
    atom_col = ((iota((SLOTS, SLOTS), 1).astype(F32) + 0.5) * (1.0 / PPA)).astype(jnp.int32)
    spread = jnp.zeros((PPA, SLOTS), F32)
    for a in range(SLOTS // PPA):
        spread += jnp.where(iota((PPA, SLOTS), 1) == iota((PPA, SLOTS), 0) + PPA * a, 1.0, 0.0)
    slot = iota((SLOTS, 128), 0)
    atom = iota((SLOTS, 128), 1) - 8 * me
    flat = jnp.zeros((SLOTS, PPA), F32)
    for p in range(PPA):
        pick = jnp.where(slot == PPA * atom + p, 1.0, 0.0)
        flat += dot(pick, 0.5 * (charges_ref[p] + charges_ref[:, p, :]), ((1,), (1,)), HIGH)
    sym[...] = jnp.where(atom_row == atom_col, dot(flat, spread, precision=HIGH), 0.0)

    colb[...] = jnp.broadcast_to(phase_ref[...], (128, 128)).T
    own = colb[pl.ds(pl.multiple_of(8 * me, 8), 8), :]
    repeat = jnp.where(((iota((SLOTS, 8), 0).astype(F32) + 0.5) * (1.0 / PPA)).astype(jnp.int32) == iota((SLOTS, 8), 1), 1.0, 0.0)
    turn[0] = jnp.where(last, dot(repeat, jnp.cos(own), precision=HIGH), 1.0)
    turn[1] = jnp.where(last, dot(repeat, jnp.sin(own), precision=HIGH), 0.0)

    forward(6, 8)
    permute_first()
    ring_end(0)

    def product(left, at, width, parts):
        total = None
        for r in range(2):
            for ref, lo, n in parts:
                term = dot(left[:, pl.ds(pl.multiple_of(at + r * width + lo, 128), n)], ref[r, 0:n, :])
                total = term if total is None else total + term
        return total

    def f_wait(lo, hi):
        for c in range(lo, hi):
            f_copy(c).wait_recv()

    plane[odd] = product(lt, kept, NPW, [(xw, 0, OWN)])
    ring_rest(1)
    ring_end(1)

    @pl.when(jnp.logical_not(first | last))
    def _():
        f_wait(0, WCH)
        plane[1 - odd] = product(lt, kept, NPW, [(yw, 0, OWN)])

    @pl.when(last)
    def _():
        f_wait(0, XCH)
        plane[1 - odd] = product(lt, kept, NPW, [(yw, 0, EXTRA)])

    @pl.when(first)
    def _():
        f_wait(0, WCH)
        for c in range(XCH):
            to_first(c).wait_recv()
        plane[1 - odd] = product(lp, 0, OWN + EXTRA, [(yw, 0, OWN), (ew, OWN, EXTRA)])

    for c in range(PARTS):
        for r in range(2):
            lo = NB * c + HALF * r
            turned = plane[1, lo : lo + HALF, :].T
            for p in range(16):
                oc[1, p % 2, p // 2, r, :, HALF * c : HALF * (c + 1)] = turned[16 * p : 16 * (p + 1)]

    def o_core(t):
        return send(oc.at[t, 1 - core], ocore.at[t], oc_s.at[t], oc_r.at[t], pw_core, ka)

    def o_copy(t, d):
        to = lax.rem(j + d, 8)
        return send(oc.at[t, core, to], orecv.at[t, d], o_s.at[t, d], o_r.at[t, d], 2 * to + core, (ka, before)[t])

    def o_start(t):
        o_core(t).wait_recv()
        for b in range(8):
            oc[t, core, b] += ocore[t, b]
        for d in range(1 - t, 8):
            o_copy(t, d).start()

    o_core(1).start()

    def rows(ref, q):
        return ref[pl.ds(q, SLOTS, stride=2), :]

    def weigh(c):
        for e in range(SUB):
            for d in range(2):
                n_copy(c, e, d).wait_recv()
        nxt[c, 0] += nxt[c, 1]
        nr = rows(nxt.at[c, 0], 0)
        ni = rows(nxt.at[c, 0], 1)
        both = jnp.concatenate([nr * turn[0] + ni * turn[1], ni * turn[0] - nr * turn[1]], axis=1)
        weighted = dot(sym[...], both, precision=HIGH)
        wr = weighted[:, :HALF]
        wi = weighted[:, HALF:]
        ket[0:SLOTS, NB * c : NB * c + HALF] = wr
        ket[0:SLOTS, NB * c + HALF : NB * (c + 1)] = wi
        ket[SLOTS:, NB * c : NB * c + HALF] = wi
        ket[SLOTS:, NB * c + HALF : NB * (c + 1)] = -wr

    def hold(c):
        for e in range(SUB):
            y_copy(c, e).wait_recv()
        pk[c] = ps[c, core, block_of(h, x)] + ydst[c]
        for q in range(2):
            bra[HALF * c : HALF * (c + 1), SLOTS * q : SLOTS * (q + 1)] = rows(pk.at[c], q).T

    hold(0)
    weigh(0)
    o_start(1)
    hold(1)
    weigh(1)
    stage[...] = dot(bra[...], ket[...], precision=HIGH)

    for p in range(16):
        at = slice(16 * p, 16 * (p + 1))
        lo = NB * (p // 8) + 16 * (p % 8)
        for c in range(PARTS):
            bands = slice(HALF * c, HALF * (c + 1))
            oc[0, p % 2, p // 2, 0, :, bands] = stage[at, NB * c : NB * c + HALF] + plane[0, lo : lo + 16, bands]
            oc[0, p % 2, p // 2, 1, :, bands] = stage[at, NB * c + HALF : NB * (c + 1)] - plane[0, lo + HALF : lo + HALF + 16, bands]
    o_core(0).start()

    o_start(0)
    result = oc[0, core, j]
    for t in (1, 0):
        for d in range(1 - t, 8):
            o_copy(t, d).wait_recv()
            result += orecv[t, d]
    for r in range(2):
        for p in range(PARTS):
            out_ref[pl.ds(2 * p + r, 16, stride=4), :] = result[r][:, HALF * p : HALF * (p + 1)]

    for t in range(2):
        o_core(t).wait_send()
        for d in range(1 - t, 8):
            o_copy(t, d).wait_send()
    for c in range(WCH):
        w_copy(c).wait_send()

    @pl.when(ka != 1)
    def _():
        for c in range(WCH):
            f_copy(c).wait_send()

    @pl.when(first)
    def _():
        for c in range(XCH):
            to_last(c).wait_send()

    @pl.when(last)
    def _():
        for c in range(XCH):
            to_first(c).wait_send()

    for c in range(PARTS):
        core_copy(c).wait_send()
        for e in range(SUB):
            y_copy(c, e).wait_send()
            for d in range(2):
                n_copy(c, e, d).wait_send()
                far_copy(c, e, d).wait_send()
                for hh in range(2):
                    near_copy(c, e, d, hh).wait_send()


def local(waves, projectors, projector_order, shift_map, charges, atom_phase):
    vmem = pl.BlockSpec(memory_space=pltpu.VMEM)
    hbm = pl.BlockSpec(memory_space=pl.ANY)
    dma = pltpu.SemaphoreType.DMA
    rows = pl.pallas_call(
        kernel,
        out_shape=jax.ShapeDtypeStruct((64, HALF), F32),
        in_specs=[vmem, vmem, vmem, vmem, hbm, hbm],
        out_specs=vmem,
        scratch_shapes=[
            pltpu.VMEM((2, NPW, NB), BF16),
            pltpu.VMEM((2 * NB, 2 * NPW), BF16),
            pltpu.VMEM((STEPS, 2, NPW, COLS), BF16),
            pltpu.VMEM((PARTS, 2 * NPROJ, 128), F32),
            pltpu.VMEM((PARTS, 2, 8, ROWS, 128), F32),
            pltpu.VMEM((PARTS, 8, ROWS, 128), F32),
            pltpu.VMEM((PARTS, 2, ROWS, 128), F32),
            pltpu.VMEM((PARTS, 2, 2, ROWS, 128), F32),
            pltpu.VMEM((PARTS, ROWS, 128), F32),
            pltpu.VMEM((PARTS, 2, ROWS, 128), F32),
            pltpu.VMEM((PARTS, ROWS, 128), F32),
            pltpu.VMEM((2, OWN, NB), BF16),
            pltpu.VMEM((2, OWN, NB), BF16),
            pltpu.VMEM((2, EXTRA, NB), BF16),
            pltpu.VMEM((2, EXTRA, NB), BF16),
            pltpu.VMEM((2 * NB, 2 * (OWN + EXTRA)), BF16),
            pltpu.VMEM((128, 128), F32),
            pltpu.VMEM((NB, COLS), F32),
            pltpu.VMEM((SLOTS, 16), jnp.int32),
            pltpu.SMEM((SLOTS, 16), jnp.int32),
            pltpu.VMEM((SLOTS, SLOTS), F32),
            pltpu.VMEM((2, SLOTS, 128), F32),
            pltpu.VMEM((NB, 2 * SLOTS), F32),
            pltpu.VMEM((2 * SLOTS, 2 * NB), F32),
            pltpu.VMEM((2, 2 * NB, NB), F32),
            pltpu.VMEM((NB, 2 * NB), F32),
            pltpu.VMEM((2, 2, 8, 2, 16, NB), F32),
            pltpu.VMEM((2, 8, 2, 16, NB), F32),
            pltpu.VMEM((2, 8, 2, 16, NB), F32),
            pltpu.VMEM((128, NPW), BF16),
            dma, dma((STEPS,)), dma,
            dma((PARTS,)), dma((PARTS,)),
            dma((PARTS, SUB, 6)), dma((PARTS, SUB, 2)), dma((PARTS, SUB, 2, 2)),
            dma((PARTS, SUB)), dma((PARTS, SUB)), dma((PARTS, SUB, 2)), dma((PARTS, SUB, 2)),
            dma((WCH,)), dma((WCH,)), dma((WCH,)), dma((WCH,)), dma((XCH,)), dma((XCH,)),
            dma((2,)), dma((2,)), dma((2, 8)), dma((2, 8)),
        ],
        compiler_params=pltpu.CompilerParams(collective_id=0, has_side_effects=True, vmem_limit_bytes=64 * 1024 * 1024 - 65536),
    )(
        projector_order.reshape(NPROJ // 128, 128),
        shift_map.reshape(NPW // 128, 128),
        atom_phase.reshape(1, 128),
        jnp.transpose(charges, (1, 2, 0)),
        waves,
        projectors,
    )
    return rows.reshape(1, 16, PARTS, 2, HALF).transpose(0, 1, 3, 2, 4).reshape(1, 16, 2, NB)


def solution(mesh):
    in_specs = (P("ka", None, "pw", None), P("ka", None, "pw", None), P(), P("pw"), P(), P())
    out_specs = P("ka", "pw", None, None)
    return jax.shard_map(local, mesh=mesh, in_specs=in_specs, out_specs=out_specs, check_vma=False)
```

time: 90.4 us -> 75.3 us (0.83)
  Pallas kernels: 86.1 us -> 73.1 us
  local copies, waits for them, and re-layouts: 3.96 us -> 1.38 us
    pallas_call x1, Pallas kernels: 86.1 us -> 73.1 us  [local(): pl.pallas_call(kernel, out_shape=jax.ShapeDtypeStruct((64, HALF), F32), i...]
    unnamed x2 -> x1, local copies, waits for them, and re-layouts: 3.96 us -> 1.38 us
where the time goes in v2:
time: 75.3 us; the launch traced here: 74.5 us
  Pallas kernels  73.1 us (97%)
  local copies, waits for them, and re-layouts  1.38 us (2%)
    pallas_call x1, Pallas kernels, local(): pl.pallas_call(kernel, out_shape=jax.ShapeDtypeStruct((64, HALF), F32), i...  73.1 us

profile of v2, /device:TPU:1, one launch (start us, length us, event | category | flops | bytes accessed | tf_op | source)
XLA Modules:
  0.0 74.5 jit_solution(5687340565313136998)
XLA Ops:
  0.0 73.1 %shard_map.64 = f32[64,128]{1,0:T(8,128)} custom-call(s32[18,128]{1,0:T(8,128)} %bitcast.11, s32[16,128]{1,0:T(8,128)} %bitcast.12, f32[1,128]{1,0:T(1,128)} %bitcast.13, f32[18,18,128]{2,1,0:T(8,128)} %bitcast.9, bf16[1,2,2048,256]{3,2,1,0:T(8,128)(2,1)} %waves_ref.1, bf16[1,2,2048,2304]{3,2,1,0:T(8,128)(2,1)} %proj_ref.1), custom_call_target="tpu_custom_call" | custom-call | tf_op jit(solution)/shard_map/pallas_call | solution.py:485
  73.1 1.4 %copy.9 = f32[1,16,2,256]{3,2,1,0:T(2,128)} copy(f32[1,16,2,256]{3,2,1,0:T(2,128)} %bitcast.10) | data formatting | bytes 65536

commit v3 on v2

--- a/solution.py
+++ b/solution.py
@@ -14,7 +14,7 @@
 NB = 256
 PPA = 18
 NPROJ = 2304
-COLS = 256
+COLS = 768
 STEPS = NPROJ // COLS
 PARTS = 2
 HALF = NB // PARTS
@@ -26,7 +26,7 @@
 WROWS = OWN // WCH
 XCH = 4
 EXTRA = OWN // 2
-SPLIT = 6
+SPLIT = 2
 
 
 def dot(a, b, dims=((1,), (0,)), precision=None):
@@ -83,8 +83,8 @@
     pw_y = pw_of(oh, x, core)
     barrier = pltpu.get_barrier_semaphore()
     peers = [(lax.rem(me + d, 16), ka) for d in range(1, 16)]
-    peers += [(me, lax.rem(ka + d, 8)) for d in (2, 6)]
-    peers += [(2 * lax.rem(j + d, 8) + core, k) for d in range(8) for k in (before, after)]
+    peers += [(me, lax.rem(ka + d, 8)) for d in (1, 2, 6, 7)]
+    peers += [(pw_y, k) for k in (before, after)]
     for peer in peers:
         pl.semaphore_signal(barrier, inc=1, device_id=peer, device_id_type=MESH)
 
@@ -98,6 +98,33 @@
     invv[...] = jnp.clip(2 * found.astype(jnp.int32), 0, 2 * (NPROJ - 1))
     inv_copy = pltpu.make_async_copy(invv, invs, inv_sem)
     inv_copy.start()
+
+    pl.semaphore_wait(barrier, len(peers))
+
+    def piece(ref, c):
+        return ref.at[:, pl.ds(c * WROWS, WROWS), :]
+
+    def w_copy(c):
+        src = waves_ref.at[0, :, pl.ds(pl.multiple_of(sent + c * WROWS, WROWS), WROWS), :]
+        return send(src, piece(xw, c), w_s.at[c], w_r.at[c], me, partner)
+
+    def f_copy(c):
+        return send(piece(xw, c), piece(yw, c), f_s.at[c], f_r.at[c], me, beyond)
+
+    def to_last(c):
+        return send(piece(es, c), piece(yw, c), e_s.at[c], f_r.at[c], me, before)
+
+    def to_first(c):
+        src = waves_ref.at[0, :, pl.ds(OWN + EXTRA + c * WROWS, WROWS), :]
+        return send(src, piece(ew, c), e_s.at[c], e_r.at[c], me, after)
+
+    for c in range(WCH):
+        w_copy(c).start()
+
+    @pl.when(last)
+    def _():
+        for c in range(XCH):
+            to_first(c).start()
 
     load.wait()
     for i in range(2, STEPS):
@@ -114,33 +141,6 @@
             lt[NB * p : NB * p + HALF, gi] = im[bands]
             lt[NB * p + HALF : NB * (p + 1), g] = im[bands]
             lt[NB * p + HALF : NB * (p + 1), gi] = -re[bands]
-
-    pl.semaphore_wait(barrier, len(peers))
-
-    def piece(ref, c):
-        return ref.at[:, pl.ds(c * WROWS, WROWS), :]
-
-    def w_copy(c):
-        src = waves_ref.at[0, :, pl.ds(pl.multiple_of(sent + c * WROWS, WROWS), WROWS), :]
-        return send(src, piece(xw, c), w_s.at[c], w_r.at[c], me, partner)
-
-    def f_copy(c):
-        return send(piece(xw, c), piece(yw, c), f_s.at[c], f_r.at[c], me, beyond)
-
-    def to_last(c):
-        return send(piece(es, c), piece(yw, c), e_s.at[c], f_r.at[c], me, before)
-
-    def to_first(c):
-        src = waves_ref.at[0, :, pl.ds(OWN + EXTRA + c * WROWS, WROWS), :]
-        return send(src, piece(ew, c), e_s.at[c], e_r.at[c], me, after)
-
-    for c in range(WCH):
-        w_copy(c).start()
-
-    @pl.when(last)
-    def _():
-        for c in range(XCH):
-            to_first(c).start()
 
     def forward(lo, hi):
         for c in range(lo, hi):
@@ -302,16 +302,17 @@
     acc[...] = jnp.zeros_like(acc)
     project(0, 0, STEPS)
     inv_copy.wait()
+    forward(0, 2)
     spread_out(0)
-    forward(0, 2)
+    forward(2, 4)
     project(1, 0, SPLIT)
     ring_start(0)
     project(1, SPLIT, STEPS)
-    forward(2, 4)
+    forward(4, 6)
     spread_out(1)
     extra_first()
     ring_rest(0)
-    forward(4, 6)
+    forward(6, 8)
     ring_start(1)
 
     atom_row = ((iota((SLOTS, SLOTS), 0).astype(F32) + 0.5) * (1.0 / PPA)).astype(jnp.int32)
@@ -333,7 +334,6 @@
     turn[0] = jnp.where(last, dot(repeat, jnp.cos(own), precision=HIGH), 1.0)
     turn[1] = jnp.where(last, dot(repeat, jnp.sin(own), precision=HIGH), 0.0)
 
-    forward(6, 8)
     permute_first()
     ring_end(0)
 
@@ -375,21 +375,27 @@
             lo = NB * c + HALF * r
             turned = plane[1, lo : lo + HALF, :].T
             for p in range(16):
-                oc[1, p % 2, p // 2, r, :, HALF * c : HALF * (c + 1)] = turned[16 * p : 16 * (p + 1)]
+                oc[1, p % 2, 2 * (p // 2 % 4) + p // 8, r, :, HALF * c : HALF * (c + 1)] = turned[16 * p : 16 * (p + 1)]
 
     def o_core(t):
         return send(oc.at[t, 1 - core], ocore.at[t], oc_s.at[t], oc_r.at[t], pw_core, ka)
 
-    def o_copy(t, d):
+    def o_copy(d):
         to = lax.rem(j + d, 8)
-        return send(oc.at[t, core, to], orecv.at[t, d], o_s.at[t, d], o_r.at[t, d], 2 * to + core, (ka, before)[t])
-
-    def o_start(t):
+        return send(oc.at[0, core, to], orecv.at[0, d], o_s.at[0, d], o_r.at[0, d], 2 * to + core, ka)
+
+    def o_add(t):
         o_core(t).wait_recv()
         for b in range(8):
             oc[t, core, b] += ocore[t, b]
-        for d in range(1 - t, 8):
-            o_copy(t, d).start()
+
+    def p_copy(d):
+        to = lax.rem(x + d, 4)
+        at = pl.ds(2 * (d - 1), 2)
+        return send(oc.at[1, core, pl.ds(2 * to, 2)], orecv.at[1, at], o_s.at[1, d], o_r.at[1, d], pw_of(h, to, core), ka)
+
+    def q_copy(d):
+        return send(oc.at[1, core, 2 * x + (h, oh)[d]], orecv.at[1, 6 + d], o_s.at[1, 4 + d], o_r.at[1, 4 + d], (me, pw_y)[d], before)
 
     o_core(1).start()
 
@@ -421,7 +427,9 @@
 
     hold(0)
     weigh(0)
-    o_start(1)
+    o_add(1)
+    for d in range(1, 4):
+        p_copy(d).start()
     hold(1)
     weigh(1)
     stage[...] = dot(bra[...], ket[...], precision=HIGH)
@@ -435,20 +443,33 @@
             oc[0, p % 2, p // 2, 1, :, bands] = stage[at, NB * c + HALF : NB * (c + 1)] - plane[0, lo + HALF : lo + HALF + 16, bands]
     o_core(0).start()
 
-    o_start(0)
+    for d in range(1, 4):
+        p_copy(d).wait_recv()
+        for hh in range(2):
+            oc[1, core, 2 * x + hh] += orecv[1, 2 * (d - 1) + hh]
+    for d in range(2):
+        q_copy(d).start()
+    o_add(0)
+    for d in range(1, 8):
+        o_copy(d).start()
     result = oc[0, core, j]
-    for t in (1, 0):
-        for d in range(1 - t, 8):
-            o_copy(t, d).wait_recv()
-            result += orecv[t, d]
+    for d in range(2):
+        q_copy(d).wait_recv()
+        result += orecv[1, 6 + d]
+    for d in range(1, 8):
+        o_copy(d).wait_recv()
+        result += orecv[0, d]
     for r in range(2):
         for p in range(PARTS):
             out_ref[pl.ds(2 * p + r, 16, stride=4), :] = result[r][:, HALF * p : HALF * (p + 1)]
 
     for t in range(2):
         o_core(t).wait_send()
-        for d in range(1 - t, 8):
-            o_copy(t, d).wait_send()
+        q_copy(t).wait_send()
+    for d in range(1, 8):
+        o_copy(d).wait_send()
+    for d in range(1, 4):
+        p_copy(d).wait_send()
     for c in range(WCH):
         w_copy(c).wait_send()
 

time: 75.3 us -> 70.7 us (0.939)
  Pallas kernels: 73.1 us -> 69.2 us
    pallas_call x1, Pallas kernels: 73.1 us -> 69.2 us  [local(): pl.pallas_call(kernel, out_shape=jax.ShapeDtypeStruct((64, HALF), F32), i...]
where the time goes in v3:
time: 70.7 us; the launch traced here: 70.6 us
  Pallas kernels  69.2 us (98%)
  local copies, waits for them, and re-layouts  1.38 us (2%)
    pallas_call x1, Pallas kernels, local(): pl.pallas_call(kernel, out_shape=jax.ShapeDtypeStruct((64, HALF), F32), i...  69.2 us

profile of v3, /device:TPU:1, one launch (start us, length us, event | category | flops | bytes accessed | tf_op | source)
XLA Modules:
  0.0 70.6 jit_solution(62066462148844131)
XLA Ops:
  0.0 69.2 %shard_map.64 = f32[64,128]{1,0:T(8,128)} custom-call(s32[18,128]{1,0:T(8,128)} %bitcast.11, s32[16,128]{1,0:T(8,128)} %bitcast.12, f32[1,128]{1,0:T(1,128)} %bitcast.13, f32[18,18,128]{2,1,0:T(8,128)} %bitcast.9, bf16[1,2,2048,256]{3,2,1,0:T(8,128)(2,1)} %waves_ref.1, bf16[1,2,2048,2304]{3,2,1,0:T(8,128)(2,1)} %proj_ref.1), custom_call_target="tpu_custom_call" | custom-call | tf_op jit(solution)/shard_map/pallas_call | solution.py:506
  69.2 1.4 %copy.9 = f32[1,16,2,256]{3,2,1,0:T(2,128)} copy(f32[1,16,2,256]{3,2,1,0:T(2,128)} %bitcast.10) | data formatting | bytes 65536

commit v4 on v3

--- a/solution.py
+++ b/solution.py
@@ -430,17 +430,19 @@
     o_add(1)
     for d in range(1, 4):
         p_copy(d).start()
-    hold(1)
-    weigh(1)
-    stage[...] = dot(bra[...], ket[...], precision=HIGH)
-
-    for p in range(16):
-        at = slice(16 * p, 16 * (p + 1))
-        lo = NB * (p // 8) + 16 * (p % 8)
-        for c in range(PARTS):
-            bands = slice(HALF * c, HALF * (c + 1))
+    def margin(c):
+        bands = slice(HALF * c, HALF * (c + 1))
+        stage[:, NB * c : NB * (c + 1)] = dot(bra[...], ket[:, NB * c : NB * (c + 1)], precision=HIGH)
+        for p in range(16):
+            at = slice(16 * p, 16 * (p + 1))
+            lo = NB * (p // 8) + 16 * (p % 8)
             oc[0, p % 2, p // 2, 0, :, bands] = stage[at, NB * c : NB * c + HALF] + plane[0, lo : lo + 16, bands]
             oc[0, p % 2, p // 2, 1, :, bands] = stage[at, NB * c + HALF : NB * (c + 1)] - plane[0, lo + HALF : lo + HALF + 16, bands]
+
+    hold(1)
+    margin(0)
+    weigh(1)
+    margin(1)
     o_core(0).start()
 
     for d in range(1, 4):

time: 70.7 us -> 71.1 us (level)
  no operation moved by 1% of the time
where the time goes in v4:
time: 71.1 us; the launch traced here: 70.9 us
  Pallas kernels  69.5 us (98%)
  local copies, waits for them, and re-layouts  1.38 us (2%)
    pallas_call x1, Pallas kernels, local(): pl.pallas_call(kernel, out_shape=jax.ShapeDtypeStruct((64, HALF), F32), i...  69.5 us

profile of v4, /device:TPU:1, one launch (start us, length us, event | category | flops | bytes accessed | tf_op | source)
XLA Modules:
  0.0 70.9 jit_solution(12682968275508872282)
XLA Ops:
  0.0 69.5 %shard_map.64 = f32[64,128]{1,0:T(8,128)} custom-call(s32[18,128]{1,0:T(8,128)} %bitcast.11, s32[16,128]{1,0:T(8,128)} %bitcast.12, f32[1,128]{1,0:T(1,128)} %bitcast.13, f32[18,18,128]{2,1,0:T(8,128)} %bitcast.9, bf16[1,2,2048,256]{3,2,1,0:T(8,128)(2,1)} %waves_ref.1, bf16[1,2,2048,2304]{3,2,1,0:T(8,128)(2,1)} %proj_ref.1), custom_call_target="tpu_custom_call" | custom-call | tf_op jit(solution)/shard_map/pallas_call | solution.py:508
  69.5 1.4 %copy.9 = f32[1,16,2,256]{3,2,1,0:T(2,128)} copy(f32[1,16,2,256]{3,2,1,0:T(2,128)} %bitcast.10) | data formatting | bytes 65536
